TPU v7x, 32 devices: a whole 2x2x4 slice. The times are simulated.
32 devices in a mesh: row: 4 (over z), col: 8 (over y, x, core).
Axes of the slice: x: 2, y: 2, z: 4, core: 2. Of those that a mesh axis runs over, the one named last changes fastest.
Arguments:
- ainv_anc: bfloat16 [12288, 12288], P('row', 'col'), may hold values from -6 to 6
- l_panel: bfloat16 [1536, 12288], P('col', 'row'), may hold values from -0.109375 to 0.109375
- diag_inv: float32 [1536, 768], P('col', 'row'), may hold values from -6 to 6
- struct_mask: int32 [2, 96], replicated, may hold values 0 or 1
- pieces: float32 [1536, 32, 128], P(('row', 'col')), may hold values from -6 to 6
- tile_owner: int32 [1536, 1], P(('row', 'col')), may hold values from 0 to 31; in each aligned block of 48 rows (0 to 47, 48 to 95, ...) at most 3 rows name the same one
Outputs:
- ainv_upper: bfloat16 [1536, 12288], P('col', 'row')
- ainv_diag: float32 [1536, 768], P('col', 'row')
- moved: float32 [3072, 32, 128], P(('row', 'col'))
Inputs may be any that keep to these rules, and one draw needn't show every extreme that they name: `tile_owner`: among the 48 pieces of one device no owner is named more than 3 times, a bound that some block reaches.
All inputs are finite; a program needn't handle non-finite values.
Results may differ from a plain program's by a relative error of at most 0.015.
Values may be sent and summed in bfloat16 or wider, within the bound.
A program may use at most 128 MiB of HBM per device.

v0:
```python
import jax
import jax.numpy as jnp
from jax import lax
from jax.sharding import PartitionSpec as P

W = 768
AB = 128
SLOT = 3


def broadcast(value, axis, root):
    mine = lax.axis_index(axis) == root
    return lax.psum(jnp.where(mine, value, jnp.zeros_like(value)), axis)


def local(ainv_anc, l_panel, diag_inv, struct_mask, pieces, tile_owner):
    row_devices = lax.axis_size("row")
    col_devices = lax.axis_size("col")
    row_index = lax.axis_index("row")
    col_index = lax.axis_index("col")
    slab_rows = l_panel.shape[0]
    local_rows = l_panel.shape[1]
    cross_width = ainv_anc.shape[1]
    group_ratio = col_devices // row_devices
    supernode = col_index * slab_rows // W
    block_count = local_rows // AB
    keep_blocks = lax.dynamic_slice(
        struct_mask, (supernode, row_index * block_count), (1, block_count)
    )
    keep_rows = (
        jnp.broadcast_to(keep_blocks[:, :, None], (1, block_count, AB)).reshape(1, local_rows) > 0
    )
    masked = jnp.where(keep_rows, l_panel, jnp.zeros_like(l_panel))
    gathered = lax.all_gather(masked, "col", axis=0, tiled=True)
    offset = col_index % group_ratio * cross_width
    own_cross = lax.dynamic_slice_in_dim(gathered, offset, cross_width, 1)
    cross_rows = broadcast(own_cross, "row", col_index // group_ratio)
    product = lax.psum_scatter(
        lax.dot_general(
            cross_rows, ainv_anc, (((1,), (1,)), ((), ())), preferred_element_type=jnp.float32
        ).astype(jnp.bfloat16),
        "col",
        scatter_dimension=0,
        tiled=True,
    ).astype(jnp.float32)
    upper_rows = jnp.where(keep_rows, -product, jnp.zeros_like(product)).astype(jnp.bfloat16)
    own_block = lax.dynamic_slice_in_dim(gathered, supernode * W, W, 0)
    diag_part = lax.dot_general(
        upper_rows, own_block, (((1,), (1,)), ((), ())), preferred_element_type=jnp.float32
    )
    summed = lax.psum_scatter(
        diag_part.astype(jnp.bfloat16), "row", scatter_dimension=1, tiled=True
    ).astype(jnp.float32)
    ainv_diag = diag_inv - summed
    devices_all = row_devices * col_devices
    owners = tile_owner[:, 0]
    onehot = (owners[:, None] == jnp.arange(devices_all, dtype=jnp.int32)[None, :]).astype(
        jnp.int32
    )
    earlier = jnp.cumsum(onehot, axis=0) - onehot
    rank_in_dest = jnp.sum(earlier * onehot, axis=1)
    slot_index = owners * SLOT + rank_in_dest
    piece_rows = pieces.shape[1]
    piece_cols = pieces.shape[2]
    buffer = (
        jnp.zeros((devices_all * SLOT, piece_rows, piece_cols), jnp.float32)
        .at[slot_index]
        .set(pieces)
    )
    shaped = buffer.reshape(devices_all, SLOT, piece_rows, piece_cols)
    arrived = lax.all_to_all(
        shaped.astype(jnp.bfloat16), ("row", "col"), split_axis=0, concat_axis=0, tiled=True
    ).astype(shaped.dtype)
    moved_pieces = arrived.reshape(devices_all * SLOT, piece_rows, piece_cols)
    return (upper_rows, ainv_diag, moved_pieces)


def solution(mesh):
    in_specs = (
        P("row", "col"),
        P("col", "row"),
        P("col", "row"),
        P(),
        P(("row", "col"), None, None),
        P(("row", "col"), None),
    )
    out_specs = (P("col", "row"), P("col", "row"), P(("row", "col"), None, None))
    return jax.shard_map(local, mesh=mesh, in_specs=in_specs, out_specs=out_specs, check_vma=False)
```

profile of v0, /device:TPU:0, one launch (start us, length us, event | category | flops | bytes accessed | tf_op | source)
XLA Modules:
  0.0 382.2 jit_solution(5946898883278234848)
XLA Ops:
  7.2 0.0 all-gather.2.cloned.1.call-start
  7.2 0.8 compare_bitcast_fusion
  8.0 0.1 broadcast_bitcast_fusion
  8.1 2.4 broadcast_select_fusion
  10.5 0.0 all-gather.2.cloned.1.call-update
  10.5 0.0 all-reduce.2.cloned.1.call-start
  10.6 61.5 %all-gather.2.cloned.1.call-done = bf16[1536,3072]{1,0:T(8,128)(2,1)} async-done(((bf16[192,3072]{1,0:T(8,128)(2,1)}), bf16[1536,3072]{1,0:T(8,128)(2,1)}) %all-gather.2.cloned.1.call-update) | async-done | bytes 9437200 | tf_op jit(solution)/shard_map/all_gather | solution.py:34
  72.1 5.4 %dynamic-slice_select_fusion = bf16[1536,1536]{1,0:T(8,128)(2,1)} fusion(bf16[1536,3072]{1,0:T(8,128)(2,1)} %all-gather.2.cloned.1.call-done, s32[]{:T(128)S(6)} %select_n.53, pred[]{:T(512)S(6)} %eq.20), kind=kLoop, calls=%fused_computation.4 | loop fusion | flops 2359296 | bytes 9437189 | tf_op jit(solution)/shard_map/jit(_where)/select_n | solution.py:13
  77.4 0.0 all-reduce.2.cloned.1.call-update
  77.5 0.0 reduce-scatter.5.cloned.1.call-start
  77.5 172.1 %all-reduce.2.cloned.1.call-done = bf16[1536,1536]{1,0:T(8,128)(2,1)} async-done(((bf16[1536,1536]{1,0:T(8,128)(2,1)}), bf16[1536,1536]{1,0:T(8,128)(2,1)}) %all-reduce.2.cloned.1.call-update) | async-done | bytes 4718608 | tf_op jit(solution)/shard_map/psum | solution.py:13
  249.6 20.5 %convolution_convert_fusion = bf16[1536,3072]{1,0:T(8,128)(2,1)} fusion(bf16[1536,1536]{1,0:T(8,128)(2,1)} %all-reduce.2.cloned.1.call-done, bf16[3072,1536]{1,0:T(8,128)(2,1)} %param.6), kind=kOutput, calls=%fused_computation.1 | convolution fusion | flops 14500233216 | bytes 23592960 | tf_op jit(solution)/shard_map/dot_general | solution.py:39
  270.1 0.0 copy-start.3
  270.1 0.0 copy-start.1
  270.1 0.0 reduce-scatter.5.cloned.1.call-update
  270.1 0.6 copy-done.3
  270.7 0.1 fusion.5
  270.8 0.1 reduce_window_sum.11
  270.9 0.2 select_reduce_fusion
  271.1 0.2 broadcast_in_dim.39
  271.2 0.0 copy-done.1
  271.3 2.0 scatter_fusion
  273.3 1.0 convert_element_type.31
  274.3 3.6 all-to-all-start
  277.9 0.0 reduce-scatter.7.cloned.1.call-start
  277.9 68.1 %reduce-scatter.5.cloned.1.call-done = bf16[192,3072]{1,0:T(8,128)(2,1)} async-done(((bf16[1536,3072]{1,0:T(8,128)(2,1)}), bf16[192,3072]{1,0:T(8,128)(2,1)}) %reduce-scatter.5.cloned.1.call-update) | async-done | bytes 1179664 | tf_op jit(solution)/shard_map/reduce_scatter | solution.py:38
  346.0 1.6 select_convert_fusion
  347.6 0.0 copy-start
  347.6 4.5 %fusion.2 = bf16[192,768]{1,0:T(8,128)(2,1)S(1)} fusion(bf16[192,3072]{1,0:T(8,128)(2,1)S(1)} %select_convert_fusion, bf16[1536,3072]{1,0:T(8,128)(2,1)} %all-gather.2.cloned.1.call-done, s32[]{:T(128)S(6)} %select_n.56), kind=kOutput, calls=%fused_computation.6 | convolution fusion | flops 906117120 | bytes 6193156 | tf_op jit(solution)/shard_map/dot_general | solution.py:48
  352.1 0.0 copy-done
  352.1 0.0 copy-start.2
  352.1 0.9 copy.9
  353.0 0.0 reduce-scatter.7.cloned.1.call-update
  353.0 0.0 all-to-all-done
  353.1 1.4 bitcast_convert_fusion
  354.5 19.5 %reduce-scatter.7.cloned.1.call-done = bf16[192,192]{1,0:T(8,128)(2,1)} async-done(((bf16[768,192]{1,0:T(8,128)(2,1)}), bf16[192,192]{1,0:T(8,128)(2,1)}) %reduce-scatter.7.cloned.1.call-update) | async-done | bytes 73744
  374.0 1.0 copy.10
  375.0 0.0 copy-done.2
  375.0 0.7 convert_subtract_fusion
  (1 shorter events, 0.0 us)
Async XLA Ops:
  7.2 64.9 %all-gather.2.cloned.1.call-start = ((), (), s32[]{:S(2)}) async-start(), calls=%async_computation.3 | async-start | bytes 10616832 | tf_op jit(solution)/shard_map/all_gather | solution.py:34
  10.5 239.1 %all-reduce.2.cloned.1.call-start = ((), (), s32[]{:S(2)}) async-start(), calls=%async_computation.4 | async-start | bytes 9437184 | tf_op jit(solution)/shard_map/psum | solution.py:13
  77.5 268.6 %reduce-scatter.5.cloned.1.call-start = ((), (), s32[]{:S(2)}) async-start(), calls=%async_computation.5 | async-start | bytes 10616832 | tf_op jit(solution)/shard_map/reduce_scatter | solution.py:38
  270.1 0.7 copy-start.3
  270.1 1.2 copy-start.1
  274.3 78.7 %all-to-all-start = ((bf16[32,3,32,128]{3,2,1,0:T(8,128)(2,1)}), bf16[32,3,32,128]{3,2,1,0:T(8,128)(2,1)S(1)}, u32[]{:S(2)}, u32[]{:S(2)}) async-start(bf16[32,3,32,128]{3,2,1,0:T(8,128)(2,1)} %bitcast.5), calls=%async_computation.1 | async-start | bytes 1572864 | tf_op jit(solution)/shard_map/all_to_all | solution.py:71
  277.9 96.1 %reduce-scatter.7.cloned.1.call-start = ((), (), s32[]{:S(2)}) async-start(), calls=%async_computation.6 | async-start | bytes 491520
  347.6 4.5 %copy-start = (bf16[192,3072]{1,0:T(8,128)(2,1)}, bf16[192,3072]{1,0:T(8,128)(2,1)S(1)}, u32[]{:S(2)}) copy-start(bf16[192,3072]{1,0:T(8,128)(2,1)S(1)} %select_convert_fusion) | copy-start | bytes 3538948
  352.1 22.9 %copy-start.2 = (f32[192,192]{1,0:T(8,128)S(1)}, f32[192,192]{1,0:T(8,128)}, u32[]{:S(2)}) copy-start(f32[192,192]{1,0:T(8,128)} %param.8) | copy-start | bytes 442372
Sparse Core Ops, SparseCore 0:
  10.6 61.4 all-gather.1
  77.6 171.9 all-reduce.1
  270.2 75.7 reduce-scatter.4
  353.2 20.7 reduce-scatter.6
where the time goes:
time: 383 us; the launch traced here: 382 us
  waiting for transfers between devices  321 us (84%)
  matrix products  25 us (7%)
  between operations  13.9 us (4%)
  other arithmetic  13.6 us (4%)
  local copies, waits for them, and re-layouts  4.82 us (1%)
    psum x1, waiting for transfers between devices, broadcast(): return lax.psum(jnp.where(mine, value, jnp.zeros_like(value)), axis)  172 us
    reduce_scatter x1, waiting for transfers between devices, local(): lax.psum_scatter(lax.dot_general(cross_rows, ainv_anc, (((1,), (1,)), (()...  68.1 us
    all_gather x1, waiting for transfers between devices, local(): gathered = lax.all_gather(masked, 'col', axis=0, tiled=True)  61.5 us
    dot_general x1, matrix products, local(): lax.dot_general(cross_rows, ainv_anc, (((1,), (1,)), ((), ())), preferred...  20.5 us
    unnamed x5, waiting for transfers between devices  19.6 us
  transfers between devices with their start and end apart: 5, of which 4 were waited for; matrix products, arithmetic and copies ran while one was open for 3% of the time, Pallas kernels for 0%

commit v1 on v0

v1 whole, which is shorter than its diff:
```python
import functools

import jax
import jax.numpy as jnp
from jax import lax
from jax.experimental import pallas as pl
from jax.experimental.pallas import tpu as pltpu
from jax.sharding import PartitionSpec as P

W = 768
AB = 128
SLOT = 3
TILES = 3
MESH = pl.DeviceIdType.MESH


def flip(index, mask):
    out = index
    bit = 1
    while bit <= mask:
        if mask & bit:
            out = out + bit - 2 * bit * ((index // bit) % 2)
        bit *= 2
    return out


def differ(a, b, size):
    out = 0
    bit = 1
    while bit < size:
        out = out + ((a // bit + b // bit) % 2) * bit
        bit *= 2
    return out


def bit_order(size):
    bits = [1 << i for i in range(size.bit_length() - 1)]
    return bits[1:][::-1] + bits[:1]


def kernel(
    R, C, x_ref, ainv_hbm, keep_ref, diag_ref, upper_ref, out_diag_ref,
    ainv_ref, zbuf, gbuf, pbuf, rbuf, dbuf, dsend, drecv,
    asem, zr, zsu, zsd, ps, pr, rs, rr, gs, gr, es, er,
):
    T, ratio, nt, cw = x_ref.shape
    n = T * nt
    LR = ratio * cw
    peers = W // n
    r = lax.axis_index("row")
    c = lax.axis_index("col")
    own = c % peers

    load = pltpu.make_async_copy(ainv_hbm, ainv_ref, asem)
    load.start()

    barrier = pltpu.get_barrier_semaphore()
    for d in range(1, R):
        pl.semaphore_signal(barrier, inc=1, device_id=((r + d) % R, c), device_id_type=MESH)
    for j in range(1, C):
        pl.semaphore_signal(barrier, inc=1, device_id=(r, flip(c, j)), device_id_type=MESH)
    pl.semaphore_wait(barrier, R + C - 2)

    def z_copy(t, g, src, step):
        sems = zsu if step > 0 else zsd
        return pltpu.make_async_remote_copy(
            src_ref=src, dst_ref=zbuf.at[t, g], send_sem=sems.at[t, g], recv_sem=zr.at[t, g],
            device_id=(r + step, c), device_id_type=MESH,
        )

    def p_copy(t, g, src):
        j = differ(c, g, C)
        return pltpu.make_async_remote_copy(
            src_ref=src, dst_ref=gbuf.at[t, j], send_sem=ps.at[t, g], recv_sem=pr.at[t, j],
            device_id=(r, g), device_id_type=MESH,
        )

    def spread(t, g, src):
        @pl.when(g == c)
        def _():
            gbuf[t, 0] = src[...]

        @pl.when(g != c)
        def _():
            p_copy(t, g, src).start()

    def z_own(t):
        for h in range(ratio):
            g = r * ratio + h
            src = x_ref.at[t, h]

            @pl.when(r + 1 < R)
            def _():
                z_copy(t, g, src, 1).start()

            @pl.when(r > 0)
            def _():
                z_copy(t, g, src, -1).start()

            spread(t, g, src)

    def z_step(t, d):
        for h in range(ratio):
            below = (r - d) * ratio + h

            @pl.when(r - d >= 0)
            def _():
                src = zbuf.at[t, below]
                z_copy(t, below, src, 1).wait_recv()

                @pl.when(r + 1 < R)
                def _():
                    z_copy(t, below, src, 1).start()

                spread(t, below, src)

            above = (r + d) * ratio + h

            @pl.when(r + d < R)
            def _():
                src = zbuf.at[t, above]
                z_copy(t, above, src, -1).wait_recv()

                @pl.when(r > 0)
                def _():
                    z_copy(t, above, src, -1).start()

                spread(t, above, src)

    def z_phase(t):
        z_own(t)
        for d in range(1, R):
            z_step(t, d)

    def g_copy(rel, bit):
        where = flip(own, rel)
        return pltpu.make_async_remote_copy(
            src_ref=x_ref if rel == 0 else dbuf.at[where], dst_ref=dbuf.at[where],
            send_sem=gs.at[(rel ^ bit)], recv_sem=gr.at[(rel ^ bit)],
            device_id=(r, flip(c, bit)), device_id_type=MESH,
        )

    gather_plan = []
    held = [0]
    for bit in bit_order(peers):
        gather_plan.append((bit, list(held)))
        held = held + [j ^ bit for j in held]

    def g_start(stage):
        bit, have = gather_plan[stage]
        for j in have:
            g_copy(j, bit).start()

    def g_wait(stage):
        bit, have = gather_plan[stage]
        for j in have:
            g_copy(j, bit).wait()

    reduce_plan = []
    live = list(range(C))
    base = 0
    bits = bit_order(C)
    for bit in bits[-1:] + bits[:-1]:
        keep = [j for j in live if not j & bit]
        reduce_plan.append((bit, keep, base))
        base += len(keep)
        live = keep

    def r_copy(t, stage, j):
        bit, keep, start = reduce_plan[stage]
        slot = start + keep.index(j & ~bit)
        return pltpu.make_async_remote_copy(
            src_ref=pbuf.at[t, j | bit], dst_ref=rbuf.at[t, slot],
            send_sem=rs.at[t, slot], recv_sem=rr.at[t, slot],
            device_id=(r, flip(c, bit)), device_id_type=MESH,
        ), slot

    def multiply(t):
        for j in range(1, C):
            pltpu.make_async_remote_copy(
                src_ref=gbuf.at[t, j], dst_ref=gbuf.at[t, j], send_sem=ps.at[t, 0],
                recv_sem=pr.at[t, j], device_id=(r, c), device_id_type=MESH,
            ).wait_recv()
        step = 256

        def body(i, carry):
            cols = pl.ds(pl.multiple_of(i * step, step), step)
            got = lax.dot_general(
                gbuf[t].reshape(C * nt, cw), ainv_ref[cols, :], (((1,), (1,)), ((), ())),
                preferred_element_type=jnp.float32,
            )
            pbuf[t, :, :, cols] = got.astype(jnp.bfloat16).reshape(C, nt, step)
            return carry

        lax.fori_loop(0, LR // step, body, 0)
        for j in reduce_plan[0][1][::-1]:
            r_copy(t, 0, j)[0].start()

    def combine(t, stage):
        bit = reduce_plan[stage + 1][0]
        keep = reduce_plan[stage][1]
        for j in sorted(keep, key=lambda v: (0 if v & bit else 1, -v)):
            copy, slot = r_copy(t, stage, j)
            copy.wait_recv()
            pbuf[t, j] = (
                pbuf[t, j].astype(jnp.float32) + rbuf[t, slot].astype(jnp.float32)
            ).astype(jnp.bfloat16)
            if j & bit:
                r_copy(t, stage + 1, j)[0].start()

    def finish(t):
        copy, slot = r_copy(t, len(reduce_plan) - 1, 0)
        copy.wait_recv()
        total = pbuf[t, 0].astype(jnp.float32) + rbuf[t, slot].astype(jnp.float32)
        upper_ref[t * nt:(t + 1) * nt, :] = jnp.where(
            keep_ref[...] > 0, -total, jnp.zeros_like(total)
        ).astype(jnp.bfloat16)

    stages = len(reduce_plan)
    z_phase(0)
    g_start(0)
    dbuf[own] = x_ref[...]
    load.wait()
    for t in range(T):
        if t + 1 < T:
            z_phase(t + 1)
        multiply(t)
        if t >= 1:
            for s in range(1, stages - 1):
                combine(t - 1, s)
        combine(t, 0)
        if t + 1 < len(gather_plan) + 0 and t < len(gather_plan):
            g_wait(t)
            g_start(t + 1)
    for s in range(1, stages - 1):
        combine(T - 1, s)
    for t in range(T - 1):
        finish(t)
    done = min(T, len(gather_plan) - 1)
    for s in range(done, len(gather_plan)):
        if s > done:
            g_start(s)
        g_wait(s)
    finish(T - 1)

    def e_copy(d):
        return pltpu.make_async_remote_copy(
            src_ref=dsend.at[d - 1], dst_ref=drecv.at[d - 1],
            send_sem=es.at[d - 1], recv_sem=er.at[d - 1],
            device_id=((r + d) % R, c), device_id_type=MESH,
        )

    def part(target):
        got = jnp.zeros((n, n), jnp.float32)
        for h in range(ratio):
            got += lax.dot_general(
                upper_ref[:, h * cw:(h + 1) * cw], dbuf[target, :, h].reshape(n, cw),
                (((1,), (1,)), ((), ())), preferred_element_type=jnp.float32,
            )
        return got

    for d in range(R - 1, 0, -1):
        dsend[d - 1] = part((r + d) % R).astype(jnp.bfloat16)
        e_copy(d).start()
    total = part(r)
    for d in range(1, R):
        e_copy(d).wait_recv()
        total = total + drecv[d - 1].astype(jnp.float32)
    out_diag_ref[...] = diag_ref[...] - total
    for d in range(1, R):
        e_copy(d).wait_send()

    for t in range(T):
        for g in range(C):
            src = zbuf.at[t, g]

            @pl.when(jnp.logical_and(r + 1 < R, r >= g // ratio))
            def _():
                z_copy(t, g, src, 1).wait_send()

            @pl.when(jnp.logical_and(r > 0, r <= g // ratio))
            def _():
                z_copy(t, g, src, -1).wait_send()

            @pl.when(c != g)
            def _():
                p_copy(t, g, src).wait_send()

        for s in range(stages):
            for j in reduce_plan[s][1]:
                r_copy(t, s, j)[0].wait_send()


def local(ainv_anc, l_panel, diag_inv, struct_mask, pieces, tile_owner):
    R = lax.axis_size("row")
    C = lax.axis_size("col")
    row_index = lax.axis_index("row")
    col_index = lax.axis_index("col")
    n, LR = l_panel.shape
    cw = ainv_anc.shape[1]
    ratio = LR // cw
    nt = n // TILES
    peers = W // n
    supernode = col_index * n // W
    block_count = LR // AB
    keep_blocks = lax.dynamic_slice(
        struct_mask, (supernode, row_index * block_count), (1, block_count)
    )
    keep_rows = jnp.broadcast_to(keep_blocks[:, :, None], (1, block_count, AB)).reshape(1, LR)
    masked = jnp.where(keep_rows > 0, l_panel, jnp.zeros_like(l_panel))
    x = masked.reshape(TILES, nt, ratio, cw).transpose(0, 2, 1, 3)

    devices_all = R * C
    owners = tile_owner[:, 0]
    onehot = (owners[:, None] == jnp.arange(devices_all, dtype=jnp.int32)[None, :]).astype(
        jnp.int32
    )
    earlier = jnp.cumsum(onehot, axis=0) - onehot
    rank_in_dest = jnp.sum(earlier * onehot, axis=1)
    slot_index = owners * SLOT + rank_in_dest
    tr, tc = pieces.shape[1:]
    buffer = jnp.zeros((devices_all * SLOT, tr, tc), jnp.float32).at[slot_index].set(pieces)
    arrived = lax.all_to_all(
        buffer.reshape(devices_all, SLOT, tr, tc).astype(jnp.bfloat16),
        ("row", "col"), split_axis=0, concat_axis=0, tiled=True,
    ).astype(jnp.float32)
    moved = arrived.reshape(devices_all * SLOT, tr, tc)

    vm = pl.BlockSpec(memory_space=pltpu.VMEM)
    bf = jnp.bfloat16
    dma = pltpu.SemaphoreType.DMA
    upper, diag = pl.pallas_call(
        functools.partial(kernel, R, C),
        out_shape=(
            jax.ShapeDtypeStruct((n, LR), bf),
            jax.ShapeDtypeStruct(diag_inv.shape, jnp.float32),
        ),
        in_specs=[vm, pl.BlockSpec(memory_space=pl.ANY), vm, vm],
        out_specs=(vm, vm),
        scratch_shapes=[
            pltpu.VMEM(ainv_anc.shape, bf),
            pltpu.VMEM((TILES, C, nt, cw), bf),
            pltpu.VMEM((TILES, C, nt, cw), bf),
            pltpu.VMEM((TILES, C, nt, LR), bf),
            pltpu.VMEM((TILES, C - 1, nt, LR), bf),
            pltpu.VMEM((peers, TILES, ratio, nt, cw), bf),
            pltpu.VMEM((R - 1, n, n), bf),
            pltpu.VMEM((R - 1, n, n), bf),
            dma,
            dma((TILES, C)),
            dma((TILES, C)),
            dma((TILES, C)),
            dma((TILES, C)),
            dma((TILES, C)),
            dma((TILES, C)),
            dma((TILES, C)),
            dma((peers,)),
            dma((peers,)),
            dma((R - 1,)),
            dma((R - 1,)),
        ],
        compiler_params=pltpu.CompilerParams(
            collective_id=0, has_side_effects=True, vmem_limit_bytes=63 * 2**20
        ),
        cost_estimate=pl.CostEstimate(
            flops=2 * C * n * LR * cw, bytes_accessed=400_000_000, transcendentals=0
        ),
        name="invert",
    )(x, ainv_anc, keep_rows, diag_inv)
    return upper, diag, moved


def solution(mesh):
    in_specs = (
        P("row", "col"),
        P("col", "row"),
        P("col", "row"),
        P(),
        P(("row", "col"), None, None),
        P(("row", "col"), None),
    )
    out_specs = (P("col", "row"), P("col", "row"), P(("row", "col"), None, None))
    return jax.shard_map(local, mesh=mesh, in_specs=in_specs, out_specs=out_specs, check_vma=False)
```

time: 383 us -> 187 us (0.49)
  waiting for transfers between devices: 321 us -> 0.01 us
  Pallas kernels: 0 us -> 166 us
  matrix products: 25 us -> 0 us
  between operations: 13.9 us -> 0.76 us
  other arithmetic: 13.6 us -> 4.99 us
    psum x1 -> x0, waiting for transfers between devices: 172 us -> none  [broadcast(): return lax.psum(jnp.where(mine, value, jnp.zeros_like(value)), axis)]
    pallas_call x0 -> x1, Pallas kernels: none -> 166 us  [local(): pl.pallas_call(functools.partial(kernel, R, C), out_shape=(jax.ShapeDtype...]
    reduce_scatter x1 -> x0, waiting for transfers between devices: 68.1 us -> none  [local(): lax.psum_scatter(lax.dot_general(cross_rows, ainv_anc, (((1,), (1,)), (()...]
    all_gather x1 -> x0, waiting for transfers between devices: 61.5 us -> none  [local(): gathered = lax.all_gather(masked, 'col', axis=0, tiled=True)]
    dot_general x2 -> x0, matrix products: 25 us -> none  [the longest x1 20.5 us: local(): lax.dot_general(cross_rows, ainv_anc, (((1,), (1,)), ((), ())), preferred...]
    unnamed x5 -> x0, waiting for transfers between devices: 19.6 us -> none
    select_n x3 -> x2, other arithmetic: 7.77 us -> 0.76 us  [the longest x1 0.67 us: local(): jnp.zeros((devices_all * SLOT, tr, tc), jnp.float32).at[slot_index]]
  transfers between devices with their start and end apart: 5 -> 1, of which waited for: 4 -> 0; matrix products, arithmetic and copies ran while one was open for 3% -> 2% of each run, Pallas kernels for 0% -> 89%
where the time goes in v1:
time: 187 us; the launch traced here: 186 us
  Pallas kernels  166 us (89%)
  starting transfers between devices  7.33 us (4%)
  local copies, waits for them, and re-layouts  6.83 us (4%)
  other arithmetic  4.99 us (3%)
    pallas_call x1, Pallas kernels, local(): pl.pallas_call(functools.partial(kernel, R, C), out_shape=(jax.ShapeDtype...  166 us
    all_to_all x1, starting transfers between devices, local(): lax.all_to_all(buffer.reshape(devices_all, SLOT, tr, tc).astype(jnp.bfloa...  7.33 us
  transfers between devices with their start and end apart: 1, of which 0 were waited for; matrix products, arithmetic and copies ran while one was open for 2% of the time, Pallas kernels for 89%

profile of v1, /device:TPU:0, one launch (start us, length us, event | category | flops | bytes accessed | tf_op | source)
XLA Modules:
  0.0 185.7 jit_solution(5639743127156179967)
XLA Ops:
  0.6 0.0 copy-start.2
  0.6 0.8 fusion
  1.4 0.1 reduce_window_sum.11
  1.5 0.8 select_reduce_fusion
  2.4 0.7 fusion.1
  3.0 0.2 broadcast_in_dim.34
  3.2 0.0 copy-done.2
  3.2 2.0 %scatter_fusion = f32[96,32,128]{2,1,0:T(8,128)S(1)} fusion(f32[96,32,128]{2,1,0:T(8,128)S(1)} %broadcast_in_dim.34, s32[48]{0:T(128)S(1)} %fusion.1, f32[48,32,128]{2,1,0:T(8,128)S(1)} %copy-done.2), kind=kCustom, calls=%fused_computation | custom fusion | bytes 2359488 | tf_op jit(solution)/shard_map/scatter | solution.py:322
  5.3 1.0 convert_element_type.11
  6.3 0.0 copy-start.4
  6.3 0.0 copy-start
  6.3 7.3 %all-to-all-start = ((bf16[32,3,32,128]{3,2,1,0:T(8,128)(2,1)}), bf16[32,3,32,128]{3,2,1,0:T(8,128)(2,1)S(1)}, u32[]{:S(2)}, u32[]{:S(2)}) async-start(bf16[32,3,32,128]{3,2,1,0:T(8,128)(2,1)} %bitcast.7), calls=%async_computation | async-start | bytes 1572864 | tf_op jit(solution)/shard_map/all_to_all | solution.py:323
  13.7 0.0 copy-done.4
  13.7 0.1 broadcast_compare_fusion
  13.8 0.1 broadcast_bitcast_fusion
  13.8 0.0 copy-done
  13.8 0.1 broadcast_select_fusion
  13.9 0.9 reshape.37
  14.8 1.2 copy.11
  16.0 0.7 broadcast_in_dim.32
  16.7 165.8 %invert.1 = (bf16[192,3072]{1,0:T(8,128)(2,1)}, f32[192,192]{1,0:T(8,128)}) custom-call(bf16[3,2,64,1536]{3,2,1,0:T(8,128)(2,1)} %bitcast.21, bf16[3072,1536]{1,0:T(8,128)(2,1)} %ainv_hbm.1, s32[1,3072]{1,0:T(1,128)} %bitcast.22, f32[192,192]{1,0:T(8,128)} %diag_ref.1), custom_call_target="tpu_custom_call" | custom-call | flops 14495514624 | bytes 400000000 | tf_op jit(solution)/shard_map/invert/pallas_call | solution.py:332
  182.5 0.0 copy-start.1
  182.5 0.0 all-to-all-done
  182.5 1.4 bitcast_convert_fusion
  183.9 0.0 copy-done.1
  184.0 0.0 copy-start.3
  184.0 1.0 copy.15
  185.0 0.1 copy-done.3
  185.1 0.7 copy.16
Async XLA Ops:
  0.6 2.6 %copy-start.2 = (f32[48,32,128]{2,1,0:T(8,128)S(1)}, f32[48,32,128]{2,1,0:T(8,128)}, u32[]{:S(2)}) copy-start(f32[48,32,128]{2,1,0:T(8,128)} %param.10) | copy-start | bytes 2359300
  6.3 7.4 %copy-start.4 = (s32[2,96]{1,0:T(2,128)S(1)}, s32[2,96]{1,0:T(2,128)}, u32[]{:S(2)}) copy-start(s32[2,96]{1,0:T(2,128)} %param.9) | copy-start | bytes 2308
  6.3 7.5 %copy-start = (bf16[192,3072]{1,0:T(8,128)(2,1)S(1)}, bf16[192,3072]{1,0:T(8,128)(2,1)}, u32[]{:S(2)}) copy-start(bf16[192,3072]{1,0:T(8,128)(2,1)} %param.7) | copy-start | bytes 3538948
  6.3 176.2 %all-to-all-start = ((bf16[32,3,32,128]{3,2,1,0:T(8,128)(2,1)}), bf16[32,3,32,128]{3,2,1,0:T(8,128)(2,1)S(1)}, u32[]{:S(2)}, u32[]{:S(2)}) async-start(bf16[32,3,32,128]{3,2,1,0:T(8,128)(2,1)} %bitcast.7), calls=%async_computation | async-start | bytes 1572864 | tf_op jit(solution)/shard_map/all_to_all | solution.py:323
  182.5 1.4 copy-start.1
  184.0 1.1 copy-start.3
